TPU v7x, 16 devices: a whole 2x2x2 slice. The times are simulated.
16 devices in a mesh: dp: 4 (over z, y), tp: 4 (over x, core).
Axes of the slice: x: 2, y: 2, z: 2, core: 2. Of those that a mesh axis runs over, the one named last changes fastest.
Arguments:
- x_in: bfloat16 [1024, 4096], P(('dp', 'tp')), parts along dimension 0
- w_in: bfloat16 [4096, 16384], P(None, 'tp')
- grad_out: bfloat16 [1024, 16384], P('dp', 'tp'), parts along dimension 0
Outputs:
- output 1: bfloat16 [1024, 4096], P(('dp', 'tp')), parts along dimension 0
- output 2: float32 [16384, 16384], P('dp', 'tp'), parts along dimension 0
There are 4 independent parts. A program takes and returns all parts, laid end to end along the dimension named above; an argument that names none is the same for every part.
All inputs are finite; a program needn't handle non-finite values.
Results may differ from a plain program's by a relative error of at most 0.001.
Values are sent between devices in bfloat16 or wider.
A program may use at most 1 GiB of HBM per device.

v0:
```python
import jax
import jax.numpy as jnp
from jax import lax
from jax.experimental import pallas as pl
from jax.experimental.pallas import tpu as pltpu
from jax.sharding import PartitionSpec as P


MESH = pl.DeviceIdType.MESH
CROSS = [(0, 2), (1, 3), (2, 0), (3, 1)]
CHUNK = 512
SLOTS = 4
PIECES = 4
EARLY = 384


def neighbours():
    me = lax.axis_index("tp")
    sib = me + 1 - 2 * lax.rem(me, 2)
    return me, lax.rem(me + 2, 4), sib, lax.rem(sib + 2, 4)


def front_kernel(x_ref, g_ref, w_ref, near_ref, far_ref, early_ref, x_all, g_all,
                 w_buf, own, send, recv, early_src,
                 x_sem, g_sem, w_sem, sum_send, sum_recv, sib_send, sib_recv,
                 cross_send, cross_recv, last_send, last_recv, early_send, early_recv):
    order = neighbours()
    _, cross, sib, _ = order
    tokens = x_ref.shape[0]
    chunks = w_ref.shape[0] // CHUNK
    piece = x_ref.shape[1] // PIECES

    def remote(src, dst, send_sem, recv_sem, to):
        return pltpu.make_async_remote_copy(
            src_ref=src, dst_ref=dst, send_sem=send_sem, recv_sem=recv_sem,
            device_id={"tp": to}, device_id_type=MESH)

    def block(j):
        return pl.ds(j * tokens, tokens)

    def chunk_of(c):
        return pl.ds(pl.multiple_of(c * CHUNK, CHUNK), CHUNK)

    fetch_x = pltpu.make_async_copy(x_ref, x_all.at[block(0)], x_sem)
    fetch_g = [
        pltpu.make_async_copy(
            g_ref.at[pl.ds(pl.multiple_of(idx * tokens, tokens), tokens)], g_all.at[block(j)], g_sem.at[j])
        for j, idx in enumerate(order)]

    def fetch_w(c):
        slot = lax.rem(c, SLOTS)
        return pltpu.make_async_copy(w_ref.at[chunk_of(c)], w_buf.at[slot], w_sem.at[slot])

    def cross_piece(p, src=x_ref):
        cols = pl.ds(p * piece, piece)
        return remote(src.at[:, cols], x_all.at[block(1), cols], cross_send.at[p], cross_recv.at[p], cross)

    def last_piece(p):
        cols = pl.ds(p * piece, piece)
        return remote(x_all.at[block(1), cols], x_all.at[block(3), cols], last_send.at[p], last_recv.at[p], sib)

    def to_sibling(c):
        return remote(send.at[c], recv.at[c], sum_send.at[c], sum_recv.at[c], sib)

    early = remote(early_src, early_ref, early_send, early_recv, cross)

    def x_to_sibling(src=x_ref):
        return remote(src, x_all.at[block(2)], sib_send, sib_recv, sib)

    def send_x(src):
        for p in range(PIECES):
            cross_piece(p, src).start()
        x_to_sibling(src).start()

    def first_reads():
        for copy in fetch_g:
            copy.start()
        fetch_w(0).start()

    upper = order[0] >= 2

    @pl.when(jnp.logical_not(upper))
    def _():
        fetch_x.start()
        first_reads()

    barrier = pltpu.get_barrier_semaphore()
    for to in (sib, cross):
        pl.semaphore_signal(barrier, inc=1, device_id={"tp": to}, device_id_type=MESH)
    pl.semaphore_wait(barrier, 2)

    @pl.when(jnp.logical_not(upper))
    def _():
        fetch_x.wait()
        send_x(x_all.at[block(0)])

    @pl.when(upper)
    def _():
        send_x(x_ref)
        first_reads()
        fetch_x.start()

    for c in range(1, SLOTS - 1):
        fetch_w(c).start()
    for copy in fetch_g:
        copy.wait()

    def forward(p):
        cross_piece(p).wait_recv()
        last_piece(p).start()

    def finish(c):
        to_sibling(c).wait_recv()
        near_ref[:, chunk_of(c)] = own[c, :tokens] + recv[c, :tokens]
        total = own[c, tokens:] + recv[c, tokens:]

        @pl.when(c == 0)
        def _():
            early_src[...] = total[:, :EARLY]
            far_ref[:, :CHUNK - EARLY] = total[:, EARLY:]

        @pl.when(c >= 1)
        def _():
            far_ref[:, pl.ds(pl.multiple_of(c * CHUNK - EARLY, 128), CHUNK)] = total

    def step(c, carry):
        fetch_w(c).wait()

        @pl.when(c + SLOTS - 1 < chunks)
        def _():
            fetch_w(c + SLOTS - 1).start()

        part = lax.dot_general(g_all[...], w_buf[lax.rem(c, SLOTS)], (((1,), (1,)), ((), ())),
                               preferred_element_type=jnp.float32)
        own[c] = part[:2 * tokens]
        send[c] = part[2 * tokens:]

        @pl.when(c >= 2)
        def _():
            finish(c - 2)

        to_sibling(c).start()
        for p, when in enumerate((2, 4, 6, 7)):
            @pl.when(c == when)
            def _():
                forward(p)

        @pl.when(c == 3)
        def _():
            early.start()

        return carry

    lax.fori_loop(0, chunks, step, 0)
    finish(chunks - 2)
    finish(chunks - 1)
    x_to_sibling().wait()

    @pl.when(upper)
    def _():
        fetch_x.wait()

    for c in range(chunks):
        to_sibling(c).wait_send()
    early.wait()
    for p in range(PIECES):
        cross_piece(p).wait_send()
        last_piece(p).wait()


def front(x, g, w):
    tokens, (hidden, ffn) = x.shape[0], w.shape
    chunks = hidden // CHUNK
    dma = pltpu.SemaphoreType.DMA
    sums = pltpu.VMEM((chunks, 2 * tokens, CHUNK), jnp.float32)
    return pl.pallas_call(
        front_kernel,
        out_shape=(
            jax.ShapeDtypeStruct((tokens, hidden), jnp.float32),
            jax.ShapeDtypeStruct((tokens, hidden - EARLY), jnp.float32),
            jax.ShapeDtypeStruct((tokens, EARLY), jnp.float32),
            jax.ShapeDtypeStruct((4 * tokens, hidden), x.dtype),
            jax.ShapeDtypeStruct(g.shape, g.dtype),
        ),
        in_specs=[pl.BlockSpec(memory_space=pl.ANY)] * 3,
        out_specs=[pl.BlockSpec(memory_space=pltpu.VMEM)] * 5,
        scratch_shapes=[
            pltpu.VMEM((SLOTS, CHUNK, ffn), w.dtype),
            sums, sums, sums,
            pltpu.VMEM((tokens, EARLY), jnp.float32),
            dma, dma((4,)), dma((SLOTS,)), dma((chunks,)), dma((chunks,)), dma, dma,
            dma((PIECES,)), dma((PIECES,)), dma((PIECES,)), dma((PIECES,)), dma, dma,
        ],
        cost_estimate=pl.CostEstimate(
            flops=2 * g.shape[0] * hidden * ffn, bytes_accessed=2 * hidden * ffn, transcendentals=0),
        compiler_params=pltpu.CompilerParams(
            collective_id=0, has_side_effects=True, vmem_limit_bytes=46 * 1024 * 1024),
        name="front",
    )(x, g, w)


def dw_kernel(x_ref, g_ref, out_ref, out_buf, out_sem):
    slots, rows = out_buf.shape[0], out_buf.shape[1]
    steps = x_ref.shape[1] // rows

    def put(i):
        return pltpu.make_async_copy(
            out_buf.at[lax.rem(i, slots)], out_ref.at[pl.ds(pl.multiple_of(i * rows, rows), rows)],
            out_sem.at[lax.rem(i, slots)])

    def step(i, carry):
        @pl.when(i >= slots)
        def _():
            put(i - slots).wait()

        out_buf[lax.rem(i, slots)] = lax.dot_general(
            x_ref[:, pl.ds(pl.multiple_of(i * rows, rows), rows)], g_ref[...],
            (((0,), (0,)), ((), ())), preferred_element_type=jnp.float32)
        put(i).start()
        return carry

    lax.fori_loop(0, steps, step, 0)
    for i in range(steps - slots, steps):
        put(i).wait()


def dw(x, g, rows=128, slots=8):
    tokens, hidden = x.shape
    ffn = g.shape[1]
    return pl.pallas_call(
        dw_kernel,
        out_shape=jax.ShapeDtypeStruct((hidden, ffn), jnp.float32),
        in_specs=[pl.BlockSpec(memory_space=pltpu.VMEM)] * 2,
        out_specs=pl.BlockSpec(memory_space=pl.ANY),
        scratch_shapes=[
            pltpu.VMEM((slots, rows, ffn), jnp.float32),
            pltpu.SemaphoreType.DMA((slots,)),
        ],
        cost_estimate=pl.CostEstimate(
            flops=2 * tokens * hidden * ffn, bytes_accessed=4 * hidden * ffn, transcendentals=0),
        compiler_params=pltpu.CompilerParams(vmem_limit_bytes=40 * 1024 * 1024),
        name="dw",
    )(x, g)


def solution(mesh):
    def per_device(x, w, g):
        x = pltpu.with_memory_space_constraint(x, pltpu.HBM)
        near, far, early, x_all, g_all = front(x, g, w)
        arrived = lax.ppermute(far, "tp", CROSS)
        grad_w = dw(x_all, g_all)
        arrived = jnp.concatenate([early, arrived], axis=1)
        return (near + arrived).astype(jnp.bfloat16), grad_w

    return jax.shard_map(
        per_device,
        mesh=mesh,
        in_specs=(P(("dp", "tp"), None), P(None, "tp"), P("dp", "tp")),
        out_specs=(P(("dp", "tp"), None), P("dp", "tp")),
        check_vma=False,
    )
```

profile of v0, /device:TPU:0, one launch (start us, length us, event | category | flops | bytes accessed | tf_op | source)
XLA Modules:
  0.0 43.0 jit_solution(15082914392270727046)
XLA Ops:
  0.6 18.6 %front.1 = (f32[64,4096]{1,0:T(8,128)S(1)}, f32[64,3712]{1,0:T(8,128)S(1)}, f32[64,384]{1,0:T(8,128)S(1)}, bf16[256,4096]{1,0:T(8,128)(2,1)S(1)}, bf16[256,4096]{1,0:T(8,128)(2,1)S(1)}) custom-call(bf16[64,4096]{1,0:T(8,128)(2,1)} %x_ref.1, bf16[256,4096]{1,0:T(8,128)(2,1)} %g_ref.1, bf16[4096,4096]{1,0:T(8,128)(2,1)} %w_ref.1), custom_call_target="tpu_custom_call" | custom-call | flops 8589934592 | bytes 33554432 | tf_op jit(solution)/shard_map/front/pallas_call | solution.py:176
  19.2 0.9 %collective-permute-start = (f32[64,3712]{1,0:T(8,128)S(1)}, f32[64,3712]{1,0:T(8,128)S(1)}, u32[]{:S(2)}, u32[]{:S(2)}) collective-permute-start(f32[64,3712]{1,0:T(8,128)S(1)} %get-tuple-element.9), channel_id=1, source_target_pairs={{0,2},{1,3},{2,0},{3,1},{4,6},{5,7},{6,4},{7,5},{8,10},{9,11},{10,... | collective-permute-start | bytes 2850824 | tf_op jit(solution)/shard_map/ppermute | solution.py:250
  20.1 21.5 %dw.1 = f32[4096,4096]{1,0:T(8,128)} custom-call(bf16[256,4096]{1,0:T(8,128)(2,1)S(1)} %get-tuple-element.10.x_ref, bf16[256,4096]{1,0:T(8,128)(2,1)S(1)} %get-tuple-element.11.g_ref), custom_call_target="tpu_custom_call" | custom-call | flops 8589934592 | bytes 67108864 | tf_op jit(solution)/shard_map/dw/pallas_call | solution.py:230
  41.6 0.5 %collective-permute-done = f32[64,3712]{1,0:T(8,128)S(1)} collective-permute-done((f32[64,3712]{1,0:T(8,128)S(1)}, f32[64,3712]{1,0:T(8,128)S(1)}, u32[]{:S(2)}, u32[]{:S(2)}) %collective-permute-start) | collective-permute-done | bytes 950304 | tf_op jit(solution)/shard_map/ppermute | solution.py:250
  42.1 0.9 %fusion = bf16[64,4096]{1,0:T(8,128)(2,1)} fusion(f32[64,4096]{1,0:T(8,128)S(1)} %get-tuple-element.7, f32[64,3712]{1,0:T(8,128)S(1)} %collective-permute-done, f32[64,384]{1,0:T(8,128)S(1)} %get-tuple-element.8), kind=kLoop, calls=%fused_computation.1 | loop fusion | flops 786432 | bytes 2621440 | tf_op jit(solution)/shard_map/convert_element_type | solution.py:253
Async XLA Ops:
  19.2 22.9 %collective-permute-start = (f32[64,3712]{1,0:T(8,128)S(1)}, f32[64,3712]{1,0:T(8,128)S(1)}, u32[]{:S(2)}, u32[]{:S(2)}) collective-permute-start(f32[64,3712]{1,0:T(8,128)S(1)} %get-tuple-element.9), channel_id=1, source_target_pairs={{0,2},{1,3},{2,0},{3,1},{4,6},{5,7},{6,4},{7,5},{8,10},{9,11},{10,... | collective-permute-start | bytes 2850824 | tf_op jit(solution)/shard_map/ppermute | solution.py:250
where the time goes:
time: 43.1 us; the launch traced here: 43 us
  Pallas kernels  40.1 us (93%)
  starting transfers between devices  0.9 us (2%)
  other arithmetic  0.89 us (2%)
  between operations  0.65 us (2%)
  waiting for transfers between devices  0.46 us (1%)
    pallas_call x1, Pallas kernels, dw(): pl.pallas_call(dw_kernel, out_shape=jax.ShapeDtypeStruct((hidden, ffn), j...  21.5 us
    pallas_call x1, Pallas kernels, front(): pl.pallas_call(front_kernel, out_shape=(jax.ShapeDtypeStruct((tokens, hid...  18.6 us
    ppermute x1, starting transfers between devices, per_device(): arrived = lax.ppermute(far, 'tp', CROSS)  0.9 us
    convert_element_type x1, other arithmetic, per_device(): return ((near + arrived).astype(jnp.bfloat16), grad_w)  0.89 us
  transfers between devices with their start and end apart: 1, of which 1 were waited for; matrix products, arithmetic and copies ran while one was open for 0% of the time, Pallas kernels for 50%

commit v1 on v0

--- a/solution.py
+++ b/solution.py
@@ -9,7 +9,7 @@
 MESH = pl.DeviceIdType.MESH
 CROSS = [(0, 2), (1, 3), (2, 0), (3, 1)]
 CHUNK = 512
-SLOTS = 4
+SLOTS = 3
 PIECES = 4
 EARLY = 384
 
@@ -100,8 +100,7 @@
         first_reads()
         fetch_x.start()
 
-    for c in range(1, SLOTS - 1):
-        fetch_w(c).start()
+    fetch_w(1).start()
     for copy in fetch_g:
         copy.wait()
 
@@ -126,18 +125,18 @@
     def step(c, carry):
         fetch_w(c).wait()
 
-        @pl.when(c + SLOTS - 1 < chunks)
-        def _():
-            fetch_w(c + SLOTS - 1).start()
+        @pl.when(c + 2 < chunks)
+        def _():
+            fetch_w(c + 2).start()
 
         part = lax.dot_general(g_all[...], w_buf[lax.rem(c, SLOTS)], (((1,), (1,)), ((), ())),
                                preferred_element_type=jnp.float32)
         own[c] = part[:2 * tokens]
         send[c] = part[2 * tokens:]
 
-        @pl.when(c >= 2)
-        def _():
-            finish(c - 2)
+        @pl.when(c >= 1)
+        def _():
+            finish(c - 1)
 
         to_sibling(c).start()
         for p, when in enumerate((2, 4, 6, 7)):
@@ -145,14 +144,13 @@
             def _():
                 forward(p)
 
-        @pl.when(c == 3)
+        @pl.when(c == 2)
         def _():
             early.start()
 
         return carry
 
     lax.fori_loop(0, chunks, step, 0)
-    finish(chunks - 2)
     finish(chunks - 1)
     x_to_sibling().wait()
 
@@ -162,10 +160,10 @@
 
     for c in range(chunks):
         to_sibling(c).wait_send()
-    early.wait()
     for p in range(PIECES):
         cross_piece(p).wait_send()
         last_piece(p).wait()
+    early.wait()
 
 
 def front(x, g, w):

time: 43.1 us -> 43.1 us (level)
  no operation moved by 1% of the time
where the time goes in v1:
time: 43.1 us; the launch traced here: 43 us
  Pallas kernels  40 us (93%)
  starting transfers between devices  0.9 us (2%)
  other arithmetic  0.89 us (2%)
  between operations  0.65 us (2%)
  waiting for transfers between devices  0.47 us (1%)
    pallas_call x1, Pallas kernels, dw(): pl.pallas_call(dw_kernel, out_shape=jax.ShapeDtypeStruct((hidden, ffn), j...  21.5 us
    pallas_call x1, Pallas kernels, front(): pl.pallas_call(front_kernel, out_shape=(jax.ShapeDtypeStruct((tokens, hid...  18.5 us
    ppermute x1, starting transfers between devices, per_device(): arrived = lax.ppermute(far, 'tp', CROSS)  0.9 us
    convert_element_type x1, other arithmetic, per_device(): return ((near + arrived).astype(jnp.bfloat16), grad_w)  0.89 us
  transfers between devices with their start and end apart: 1, of which 1 were waited for; matrix products, arithmetic and copies ran while one was open for 0% of the time, Pallas kernels for 50%

profile of v1, /device:TPU:0, one launch (start us, length us, event | category | flops | bytes accessed | tf_op | source)
XLA Modules:
  0.0 43.0 jit_solution(15837826045513206377)
XLA Ops:
  0.6 18.5 %front.1 = (f32[64,4096]{1,0:T(8,128)S(1)}, f32[64,3712]{1,0:T(8,128)S(1)}, f32[64,384]{1,0:T(8,128)S(1)}, bf16[256,4096]{1,0:T(8,128)(2,1)S(1)}, bf16[256,4096]{1,0:T(8,128)(2,1)S(1)}) custom-call(bf16[64,4096]{1,0:T(8,128)(2,1)} %x_ref.1, bf16[256,4096]{1,0:T(8,128)(2,1)} %g_ref.1, bf16[4096,4096]{1,0:T(8,128)(2,1)} %w_ref.1), custom_call_target="tpu_custom_call" | custom-call | flops 8589934592 | bytes 33554432 | tf_op jit(solution)/shard_map/front/pallas_call | solution.py:174
  19.2 0.9 %collective-permute-start = (f32[64,3712]{1,0:T(8,128)S(1)}, f32[64,3712]{1,0:T(8,128)S(1)}, u32[]{:S(2)}, u32[]{:S(2)}) collective-permute-start(f32[64,3712]{1,0:T(8,128)S(1)} %get-tuple-element.9), channel_id=1, source_target_pairs={{0,2},{1,3},{2,0},{3,1},{4,6},{5,7},{6,4},{7,5},{8,10},{9,11},{10,... | collective-permute-start | bytes 2850824 | tf_op jit(solution)/shard_map/ppermute | solution.py:248
  20.1 21.5 %dw.1 = f32[4096,4096]{1,0:T(8,128)} custom-call(bf16[256,4096]{1,0:T(8,128)(2,1)S(1)} %get-tuple-element.10.x_ref, bf16[256,4096]{1,0:T(8,128)(2,1)S(1)} %get-tuple-element.11.g_ref), custom_call_target="tpu_custom_call" | custom-call | flops 8589934592 | bytes 67108864 | tf_op jit(solution)/shard_map/dw/pallas_call | solution.py:228
  41.6 0.5 %collective-permute-done = f32[64,3712]{1,0:T(8,128)S(1)} collective-permute-done((f32[64,3712]{1,0:T(8,128)S(1)}, f32[64,3712]{1,0:T(8,128)S(1)}, u32[]{:S(2)}, u32[]{:S(2)}) %collective-permute-start) | collective-permute-done | bytes 950304 | tf_op jit(solution)/shard_map/ppermute | solution.py:248
  42.1 0.9 %fusion = bf16[64,4096]{1,0:T(8,128)(2,1)} fusion(f32[64,4096]{1,0:T(8,128)S(1)} %get-tuple-element.7, f32[64,3712]{1,0:T(8,128)S(1)} %collective-permute-done, f32[64,384]{1,0:T(8,128)S(1)} %get-tuple-element.8), kind=kLoop, calls=%fused_computation.1 | loop fusion | flops 786432 | bytes 2621440 | tf_op jit(solution)/shard_map/convert_element_type | solution.py:251
Async XLA Ops:
  19.2 22.9 %collective-permute-start = (f32[64,3712]{1,0:T(8,128)S(1)}, f32[64,3712]{1,0:T(8,128)S(1)}, u32[]{:S(2)}, u32[]{:S(2)}) collective-permute-start(f32[64,3712]{1,0:T(8,128)S(1)} %get-tuple-element.9), channel_id=1, source_target_pairs={{0,2},{1,3},{2,0},{3,1},{4,6},{5,7},{6,4},{7,5},{8,10},{9,11},{10,... | collective-permute-start | bytes 2850824 | tf_op jit(solution)/shard_map/ppermute | solution.py:248
